TPU v7x, 128 devices: a whole 4x4x4 slice. The times are simulated.
128 devices in a mesh: seq: 4 (over z_lo, core), ctx: 32 (over y, x, z_hi).
Axes of the slice: x: 4, y: 4, z: 4 (z_hi: 2, z_lo: 2; z = z_hi * 2 + z_lo), core: 2. Of those that a mesh axis runs over, the one named last changes fastest.
Arguments:
- hidden: bfloat16 [131072, 7168], P(('seq', 'ctx')), may hold values from -24 to 24
- router_weight: bfloat16 [7168, 256], replicated, may hold values from -0.0625 to 0.0625
- expert_index: int32 [131072, 8], P(('seq', 'ctx')), may hold values from 0 to 255, all different within a row
- lengths: int32 [4], P('seq'), may hold values from 16384 to 32768
Outputs:
- router_grad: float32 [7168, 256], P('ctx')
- balance: float32 [4], P('seq')
Inputs may be any that keep to these rules, and one draw needn't show every extreme that they name: A sequence's valid tokens are its first lengths[s] slots, the rest are padding. `expert_index`: each row names 8 different experts.
All inputs are finite; a program needn't handle non-finite values.
Results may differ from a plain program's by a relative error of at most 0.0003.
Values sent between devices are 32-bit elements; how exact they have to be, the bound alone decides.
A program may use at most 128 MiB of HBM per device.

v0:
```python
import jax
import jax.numpy as jnp
from jax import lax
from jax.sharding import Mesh
from jax.sharding import PartitionSpec as P

E = 256
TOPK = 8
CTX = ("ctx_0", "ctx_1", "ctx_2")
SEQ_CTX = ("seq", "ctx_0", "ctx_1", "ctx_2")


loss_scale = 65536.0


def copy_for_each(array, axis):
    size = lax.axis_size(axis)
    return lax.all_to_all(
        jnp.broadcast_to(array[None], (size, *array.shape)), axis, 0, 0, tiled=True
    )


def over_copies(array, axis):
    return copy_for_each(array, axis).sum(axis=0)


def in_one(arrays, axis):
    ravelled, at, finished = (jnp.concatenate([a.reshape(-1) for a in arrays]), 0, [])
    running = over_copies(ravelled, axis)
    for a in arrays:
        finished.append(running[at : at + a.size].reshape(a.shape))
        at += a.size
    return tuple(finished)


def sum_by_axis(running, axes):
    for axis in axes:
        running = lax.psum_scatter(running, axis, scatter_dimension=0, tiled=True)
    return running


def shards(hidden, router_weight, expert_index, lengths):
    tok_rows = hidden.shape[0]
    length_here = lengths[0]
    tokens_live = length_here.astype(jnp.float32)
    positions = lax.axis_index(CTX) * tok_rows + jnp.arange(tok_rows, dtype=jnp.int32)
    valid_mask = (positions < length_here).astype(jnp.float32)
    expert_ids = jnp.arange(E, dtype=jnp.int32)
    expert_hits = jnp.sum((expert_index[:, :, None] == expert_ids).astype(jnp.float32), axis=1)
    counts_local = jnp.sum(valid_mask[:, None] * expert_hits, axis=0)
    logits = jnp.dot(hidden, router_weight, preferred_element_type=jnp.float32)
    scores = jax.nn.sigmoid(logits)
    row_total = jnp.sum(scores, axis=1, keepdims=True)
    share_of = scores / row_total
    score_local = jnp.sum(valid_mask[:, None] * share_of, axis=0)
    counts_all, score_all = in_one((counts_local, score_local), CTX)
    fraction = E * counts_all / (TOPK * tokens_live)
    mean_score = score_all / tokens_live
    balance = jnp.sum(fraction * mean_score).reshape(1)
    weights = loss_scale * fraction / tokens_live
    weighted = jnp.sum(weights * share_of, axis=1, keepdims=True)
    grad_logits = (weights - weighted) / row_total * scores * (1.0 - scores) * valid_mask[:, None]
    columns = hidden.astype(jnp.float32)
    partial_rows = sum_by_axis(
        lax.dot_general(
            columns,
            grad_logits,
            (((0,), (0,)), ((), ())),
            precision=lax.Precision.HIGHEST,
            preferred_element_type=jnp.float32,
        ),
        CTX,
    )
    router_grad = over_copies(partial_rows, "seq")
    return (router_grad, balance)


def solution(mesh):
    finer = Mesh(
        mesh.devices.reshape(mesh.shape["seq"], 4, 4, 2), ("seq", "ctx_0", "ctx_1", "ctx_2")
    )
    placed = (P(SEQ_CTX, None), P(), P(SEQ_CTX, None), P("seq"))
    return jax.shard_map(
        shards, mesh=finer, in_specs=placed, out_specs=(P(CTX, None), P("seq")), check_vma=False
    )
```

profile of v0, /device:TPU:1, one launch (start us, length us, event | category | flops | bytes accessed | tf_op | source)
XLA Modules:
  0.0 211.5 jit_solution(6071089642755106362)
XLA Ops:
  7.8 1.0 copy.13
  8.8 10.9 %convert_reduce_fusion = f32[1024,256]{1,0:T(8,128)S(1)} fusion(s32[1024,8]{1,0:T(8,128)S(1)} %copy.13), kind=kLoop, calls=%fused_computation.1 | loop fusion | flops 6029312 | bytes 1081344 | tf_op jit(solution)/shard_map/reduce_sum | solution.py:49
  19.6 0.3 copy.14
  20.0 8.7 %fusion.13 = (f32[1024]{0:T(1024)S(1)}, f32[1024,256]{0,1:T(8,128)S(1)}) fusion(bf16[1024,7168]{1,0:T(8,128)(2,1)} %param.4, bf16[7168,256]{1,0:T(8,128)(2,1)} %param.5), kind=kOutput, calls=%fused_computation.22 | convolution fusion | flops 3759143936 | bytes 19402752 | tf_op jit(solution)/shard_map/dot_general | solution.py:51
  28.7 0.3 multiply_reduce_fusion.2
  29.0 0.7 broadcast_in_dim.4
  29.7 11.2 %all-to-all-start = ((f32[32,1,512]{2,1,0:T(1,128)}), f32[32,1,512]{2,1,0:T(1,128)S(1)}, u32[]{:S(2)}, u32[]{:S(2)}) async-start(f32[32,1,512]{2,1,0:T(1,128)} %broadcast_in_dim.4), calls=%async_computation | async-start | bytes 131072 | tf_op jit(solution)/shard_map/all_to_all | solution.py:18
  40.8 0.0 reduce-scatter.8.cloned.1.call-start
  40.9 8.7 %all-to-all-done = f32[32,1,512]{2,1,0:T(1,128)S(1)} async-done(((f32[32,1,512]{2,1,0:T(1,128)}), f32[32,1,512]{2,1,0:T(1,128)S(1)}, u32[]{:S(2)}, u32[]{:S(2)}) %all-to-all-start) | async-done | bytes 65568 | tf_op jit(solution)/shard_map/all_to_all | solution.py:18
  49.6 0.1 reduce_sum.76
  49.6 0.6 fusion.15
  50.2 0.2 multiply_reduce_fusion
  50.5 17.3 %convolution_bitcast_fusion = f32[7168,256]{0,1:T(8,128)} fusion(bf16[1024,7168]{1,0:T(8,128)(2,1)} %param.4, f32[1024]{0:T(1024)S(1)} %multiply_reduce_fusion, f32[256]{0:T(256)S(1)} %multiply_divide_fusion.1, f32[1024]{0:T(1024)S(1)} %get-tuple-element.6, f32[1024]{0:T(1024)S(1)} %fusion.14, f32[1024,256]{0,1:T(8,128)S(1)} %get-tuple-element.7), kind=kOutput, calls=%fused_computation | convolution fusion | flops 22550413312 | bytes 23081984 | tf_op jit(solution)/shard_map/dot_general | solution.py:65
  67.8 0.0 reduce-scatter.8.cloned.1.call-update
  67.8 0.0 reduce-scatter.10.cloned.1.call-start
  67.9 69.8 %reduce-scatter.8.cloned.1.call-done = f32[1792,256]{0,1:T(8,128)} async-done(((f32[7168,256]{0,1:T(8,128)}), f32[1792,256]{0,1:T(8,128)}) %reduce-scatter.8.cloned.1.call-update) | async-done | bytes 1835024 | tf_op jit(solution)/shard_map/reduce_scatter | solution.py:38
  137.7 2.8 %copy.17 = f32[1792,256]{1,0:T(8,128)} copy(f32[1792,256]{0,1:T(8,128)} %reduce-scatter.8.cloned.1.call-done) | data formatting | bytes 3670016
  140.5 0.0 reduce-scatter.10.cloned.1.call-update
  140.5 0.0 reduce-scatter.12.cloned.1.call-start
  140.5 27.3 %reduce-scatter.10.cloned.1.call-done = f32[448,256]{1,0:T(8,128)} async-done(((f32[1792,256]{1,0:T(8,128)}), f32[448,256]{1,0:T(8,128)}) %reduce-scatter.10.cloned.1.call-update) | async-done | bytes 458768
  167.9 0.0 reduce-scatter.12.cloned.1.call-update
  167.9 20.1 %reduce-scatter.12.cloned.1.call-done = f32[224,256]{1,0:T(8,128)} async-done(((f32[448,256]{1,0:T(8,128)}), f32[224,256]{1,0:T(8,128)}) %reduce-scatter.12.cloned.1.call-update) | async-done | bytes 229392 | tf_op jit(solution)/shard_map/reduce_scatter | solution.py:38
  188.0 1.0 broadcast_in_dim.5
  189.0 15.2 %all_to_all.11 = f32[4,224,256]{2,1,0:T(8,128)S(1)} all-to-all(f32[4,224,256]{2,1,0:T(8,128)S(1)} %broadcast_in_dim.5), channel_id=1, replica_groups=mesh['seq'=4,'ctx_0'=4,'ctx_1'=4,'ctx_2'=2] {'seq'}, dimensions={0} | all-to-all | bytes 1835008 | tf_op jit(solution)/shard_map/all_to_all | solution.py:18
  204.3 0.7 reduce_sum.78
  (3 shorter events, 0.0 us)
Async XLA Ops:
  29.7 19.9 %all-to-all-start = ((f32[32,1,512]{2,1,0:T(1,128)}), f32[32,1,512]{2,1,0:T(1,128)S(1)}, u32[]{:S(2)}, u32[]{:S(2)}) async-start(f32[32,1,512]{2,1,0:T(1,128)} %broadcast_in_dim.4), calls=%async_computation | async-start | bytes 131072 | tf_op jit(solution)/shard_map/all_to_all | solution.py:18
  40.8 96.8 %reduce-scatter.8.cloned.1.call-start = ((), (), s32[]{:S(2)}) async-start(), calls=%async_computation.5 | async-start | bytes 9175040 | tf_op jit(solution)/shard_map/reduce_scatter | solution.py:38
  67.8 100.0 %reduce-scatter.10.cloned.1.call-start = ((), (), s32[]{:S(2)}) async-start(), calls=%async_computation.6 | async-start | bytes 2293760
  140.5 47.5 %reduce-scatter.12.cloned.1.call-start = ((), (), s32[]{:S(2)}) async-start(), calls=%async_computation.7 | async-start | bytes 688128 | tf_op jit(solution)/shard_map/reduce_scatter | solution.py:38
Sparse Core Ops, SparseCore 0:
  68.0 69.6 reduce-scatter.7
  140.6 27.2 reduce-scatter.9
  170.2 17.7 reduce-scatter.11
where the time goes:
time: 212 us
  waiting for transfers between devices  126 us (59%)
  matrix products  26 us (12%)
  blocking collectives  15.2 us (7%)
  between operations  14.5 us (7%)
  other arithmetic  12.8 us (6%)
  starting transfers between devices  11.3 us (5%)
  local copies, waits for them, and re-layouts  5.72 us (3%)
    reduce_scatter x2, waiting for transfers between devices, sum_by_axis(): running = lax.psum_scatter(running, axis, scatter_dimension=0, tiled=True)  89.9 us
    unnamed x4, waiting for transfers between devices  27.4 us
    dot_general x1, matrix products, shards(): lax.dot_general(columns, grad_logits, (((0,), (0,)), ((), ())), precision...  17.3 us
    all_to_all x1, blocking collectives, copy_for_each(): lax.all_to_all(jnp.broadcast_to(array[None], (size, *array.shape)), axis,...  15.2 us
    all_to_all x1, starting transfers between devices, copy_for_each(): lax.all_to_all(jnp.broadcast_to(array[None], (size, *array.shape)), axis,...  11.2 us
    reduce_sum x1, other arithmetic, shards(): jnp.sum((expert_index[:, :, None] == expert_ids).astype(jnp.float32), axi...  10.9 us
    all_to_all x1, waiting for transfers between devices, copy_for_each(): lax.all_to_all(jnp.broadcast_to(array[None], (size, *array.shape)), axis,...  8.67 us
    dot_general x1, matrix products, shards(): logits = jnp.dot(hidden, router_weight, preferred_element_type=jnp.float32)  8.66 us
  transfers between devices with their start and end apart: 4, of which 4 were waited for; matrix products, arithmetic and copies ran while one was open for 0% of the time, Pallas kernels for 0%

commit v1 on v0

v1 whole, which is shorter than its diff:
```python
import jax
import jax.numpy as jnp
from jax import lax
from jax.experimental import pallas as pl
from jax.experimental.pallas import tpu as pltpu
from jax.sharding import PartitionSpec as P

D = 7168
E = 256
TOPK = 8
ROWS = 1024
BLOCK = 224
HALF = BLOCK // 2
CHUNK = 4 * BLOCK
LOSS_SCALE = 65536.0
MESH = pl.DeviceIdType.MESH

TILES = (3, 2, 2, 3, 2, 2)
OFFSET = (0, 24, 40, 56, 80, 96)
LEAD = ((64,), (4, 8, 2), (2, 8, 4), (8, 8), (4, 8, 2), (2, 8, 4))

HCH = 4
HROWS = ROWS // HCH


def place(s, j, b):
    return (
        (j * 8 + b,),
        (j % 4, b, j // 4),
        (j % 2, b, j // 2),
        (b, j),
        (b % 4, j, b // 4),
        (b % 2, j, b // 2),
    )[s]


def first_send(s, j):
    return (
        (pl.ds(j * 8, 8),),
        (j % 4, slice(None), j // 4),
        (j % 2, slice(None), j // 2),
        (pl.ds(4, 4), j),
        (pl.ds(2, 2), j, slice(None)),
        (1, j, slice(None)),
    )[s]


def span(lead, start, size):
    inner = 1
    for n in lead[1:]:
        inner *= n
    if size >= inner or len(lead) == 1:
        return (pl.ds(start // inner, size // inner),) + (slice(None),) * (len(lead) - 1)
    return (start // inner,) + span(lead[1:], start % inner, size)


def kernel(hid, wt, eidx, lens, out, bal, *scratch):
    (h, w, idx, length, share, coef, ghi, glo, own, snd, got) = scratch[:11]
    acc, rb = scratch[11:17], scratch[17:23]
    (fin, ar, in_sem, d2d_s, d2d_r, cube_s, cube_r, ar_s, ar_r, fin_s, fin_r) = scratch[23:]

    seq, ctx = lax.axis_index("seq"), lax.axis_index("ctx")
    core, zlo = seq % 2, seq // 2
    zh, x, y = ctx % 2, (ctx // 2) % 4, ctx // 8

    def device(y_, x_, zh_, zlo_, core_):
        return (zlo_ * 2 + core_, (y_ * 4 + x_) * 2 + zh_)

    cube = (
        device(3 - y, x, zh, zlo, core),
        device(y + 1 - 2 * (y % 2), x, zh, zlo, core),
        device(y, 3 - x, zh, zlo, core),
        device(y, x + 1 - 2 * (x % 2), zh, zlo, core),
        device(y, x, 1 - zh, 1 - zlo, core),
        device(y, x, zh, 1 - zlo, core),
    )
    other = device(y, x, zh, zlo, 1 - core)
    cross = device(y, x, zh, 1 - zlo, 1 - core)
    ring_x = [device(y, (x + d) % 4, zh, zlo, core) for d in (1, 2, 3)]
    ring_y = [device((y + d) % 4, x, zh, zlo, core) for d in (1, 2, 3)]
    pair_z = [device(y, x, 1 - zh, zlo, core)]
    stages = ((ring_x, x), (ring_y, y), (pair_z, zh))

    barrier = pltpu.get_barrier_semaphore()
    greeted = ring_x + ring_y + pair_z + [cube[4], cube[5], other, cross]
    for peer in greeted:
        pl.semaphore_signal(barrier, inc=1, device_id=peer, device_id_type=MESH)

    load_len = pltpu.make_async_copy(lens, length, in_sem.at[0])
    load_idx = pltpu.make_async_copy(eidx, idx, in_sem.at[1])
    load_w = pltpu.make_async_copy(wt, w, in_sem.at[2])
    load_h = [
        pltpu.make_async_copy(hid.at[pl.ds(c * HROWS, HROWS)], h.at[pl.ds(c * HROWS, HROWS)], in_sem.at[3 + c])
        for c in range(HCH)
    ]
    load_len.start()
    load_idx.start()
    load_w.start()
    for c in range(HCH):
        load_h[c].start()

    load_len.wait()
    load_idx.wait()
    live = length[0]
    first = ctx * ROWS

    def count(i, total):
        r0 = pl.multiple_of(i * 64, 64)
        block = idx[pl.ds(r0, 64), :]
        position = first + r0 + lax.broadcasted_iota(jnp.int32, block.shape, 0)
        block = jnp.where(position < live, block, -1)
        experts = lax.broadcasted_iota(jnp.int32, (64, E), 1)
        hits = jnp.zeros((64, E), jnp.float32)
        for k in range(TOPK):
            hits = hits + jnp.where(block[:, k : k + 1] == experts, 1.0, 0.0)
        return total + hits.reshape(8, 8, E).sum(axis=0)

    counts = lax.fori_loop(0, ROWS // 64, count, jnp.zeros((8, E), jnp.float32))

    def ar_copy(kind, stage, peer, where):
        return pltpu.make_async_remote_copy(
            src_ref=ar.at[(kind, stage) + where],
            dst_ref=ar.at[(kind, stage) + where],
            send_sem=ar_s.at[kind, stage],
            recv_sem=ar_r.at[kind, stage],
            device_id=peer,
            device_id_type=MESH,
        )

    def ar_send(kind, stage, value):
        peers, mine = stages[stage]
        ar[kind, stage, mine] = value
        for peer in peers:
            ar_copy(kind, stage, peer, (mine,)).start()

    def ar_wait(kind, stage):
        peers, _ = stages[stage]
        n = len(peers)
        ar_copy(kind, stage, peers[0], (pl.ds(0, n),)).wait()
        total = ar[kind, stage, 0]
        for i in range(1, n + 1):
            total = total + ar[kind, stage, i]
        return total

    pl.semaphore_wait(barrier, len(greeted))
    ar_send(0, 0, counts)

    load_w.wait()
    score_sum = jnp.zeros((8, E), jnp.float32)
    for c in range(HCH):
        rows = pl.ds(c * HROWS, HROWS)
        load_h[c].wait()
        logits = jnp.dot(h[rows, :], w[...], preferred_element_type=jnp.float32)
        scores = jax.nn.sigmoid(logits)
        row_total = jnp.sum(scores, axis=1, keepdims=True)
        position = first + c * HROWS + lax.broadcasted_iota(jnp.int32, (HROWS, 1), 0)
        valid = jnp.where(position < live, 1.0, 0.0)
        part = scores / row_total
        share[rows, :] = part
        coef[rows, :] = part * (1.0 - scores) * valid
        score_sum = score_sum + (part * valid).reshape(HROWS // 8, 8, E).sum(axis=0)
        if c == 0:
            counts = ar_wait(0, 0)
            ar_send(0, 1, counts)
        if c == 2:
            counts = ar_wait(0, 1)
            ar_send(0, 2, counts)
    counts = ar_wait(0, 2)
    ar_send(1, 0, score_sum)

    tokens = live.astype(jnp.float32)
    fraction = E * jnp.sum(counts, axis=0, keepdims=True) / (TOPK * tokens)
    weights = LOSS_SCALE * fraction / tokens
    for c in range(HCH):
        rows = pl.ds(c * HROWS, HROWS)
        weighted = jnp.sum(weights * share[rows, :], axis=1, keepdims=True)
        grad = (weights - weighted) * coef[rows, :]
        high = grad.astype(jnp.bfloat16)
        low = (grad - high.astype(jnp.float32)).astype(jnp.bfloat16)
        for e in range(2):
            columns = pl.ds(pl.multiple_of(((core + e) % 2) * 128, 128), 128)
            ghi[rows, columns] = high[:, e * 128 : (e + 1) * 128]
            glo[rows, columns] = low[:, e * 128 : (e + 1) * 128]

    def d2d(j):
        return pltpu.make_async_remote_copy(
            src_ref=snd.at[j], dst_ref=got.at[j], send_sem=d2d_s.at[j], recv_sem=d2d_r.at[j],
            device_id=other, device_id_type=MESH,
        )

    def halving(s, k, where):
        return pltpu.make_async_remote_copy(
            src_ref=acc[s].at[where], dst_ref=rb[s].at[where], send_sem=cube_s.at[s, k], recv_sem=cube_r.at[s, k],
            device_id=cube[(s + k) % 6], device_id_type=MESH,
        )

    yhi, xhi = y // 2, x // 2
    ylo, xlo = (yhi + y) % 2, (xhi + x) % 2
    v = (zh + zlo) % 2

    def multiply(j):
        y_hi = (yhi + j // 4) % 2
        y_at = 2 * y_hi + (y_hi + ylo + (j // 2) % 2) % 2
        x_hi = (xhi + j) % 2
        start = (y_at * 2 + x_hi) * CHUNK
        for m in range(CHUNK // 128):
            part = h[:, pl.ds(pl.multiple_of(start + m * 128, 128), 128)]
            dims = (((0,), (0,)), ((), ()))
            made = lax.dot_general(part, ghi[...], dims, preferred_element_type=jnp.float32)
            made = made + lax.dot_general(part, glo[...], dims, preferred_element_type=jnp.float32)
            at = m * 128
            while at < (m + 1) * 128:
                to = min((at // HALF + 1) * HALF, (m + 1) * 128)
                piece = at // HALF
                b1 = (x_hi + piece // 4 + xlo) % 2
                b2 = (piece // 2 % 2 + zh) % 2
                b3 = (piece % 2 + v) % 2
                b = b1 * 4 + b2 * 2 + b3
                lo, size = at - piece * HALF, to - at
                own[j, b, lo : lo + size] = made[at - m * 128 : to - m * 128, :128]
                snd[j, b, lo : lo + size] = made[at - m * 128 : to - m * 128, 128:]
                at = to
        d2d(j).start()

    def gather(j):
        d2d(j).wait_recv()
        for b in range(8):
            total = own[j, b] + got[j, b]
            for s in range(6):
                acc[s][place(s, j, b)] = total[OFFSET[s] : OFFSET[s] + 8 * TILES[s]]
        for s in range(3, 6):
            halving(s, 0, first_send(s, j)).start()
        for s, bit in ((0, j // 4), (1, (j // 2) % 2), (2, j % 2)):

            @pl.when(bit == 1)
            def _(s=s):
                halving(s, 0, first_send(s, j)).start()

    def step(i, carry):
        @pl.when(i < 8)
        def _():
            multiply(7 - i)

        @pl.when(i > 0)
        def _():
            gather(8 - i)

        return carry

    lax.fori_loop(0, 9, step, 0)

    score_sum = ar_wait(1, 0)
    ar_send(1, 1, score_sum)

    for k in range(6):
        n = 32 >> k
        for s in range(6):
            halving(s, k, span(LEAD[s], n, n)).wait_recv()
            low_half, high_half = span(LEAD[s], 0, n), span(LEAD[s], n, n)
            acc[s][low_half] = acc[s][low_half] + rb[s][high_half]
            if k < 5:
                halving(s, k + 1, span(LEAD[s], n // 2, n // 2)).start()
        if k == 2:
            score_sum = ar_wait(1, 1)
            ar_send(1, 2, score_sum)

    for s in range(6):
        zero = (0,) * len(LEAD[s])
        fin[core, v, OFFSET[s] : OFFSET[s] + 8 * TILES[s]] = acc[s][zero]

    last = [
        pltpu.make_async_remote_copy(
            src_ref=fin.at[core, v], dst_ref=fin.at[core, v], send_sem=fin_s.at[i], recv_sem=fin_r.at[i],
            device_id=peer, device_id_type=MESH,
        )
        for i, peer in enumerate((cube[5], cross, other))
    ]
    for copy in last:
        copy.start()

    score_sum = ar_wait(1, 2)
    mean_score = jnp.sum(score_sum, axis=0, keepdims=True) / tokens
    bal[0] = jnp.sum(fraction * mean_score)

    for k in range(6):
        for s in range(6):
            halving(s, k, span(LEAD[s], 32 >> k, 32 >> k)).wait_send()
    for j in range(8):
        d2d(j).wait_send()
    for copy in last:
        copy.wait()
    for e in range(2):
        for half in range(2):
            out[half * HALF : (half + 1) * HALF, e * 128 : (e + 1) * 128] = fin[e, half]


def solution(mesh):
    def shards(hidden, router_weight, expert_index, lengths):
        any_space = pl.BlockSpec(memory_space=pl.ANY)
        pieces = [lead + (8 * t, 128) for lead, t in zip(LEAD, TILES)]
        return pl.pallas_call(
            kernel,
            out_shape=(jax.ShapeDtypeStruct((BLOCK, E), jnp.float32), jax.ShapeDtypeStruct((1,), jnp.float32)),
            in_specs=[any_space] * 4,
            out_specs=(pl.BlockSpec(memory_space=pltpu.VMEM), pl.BlockSpec(memory_space=pltpu.SMEM)),
            scratch_shapes=[
                pltpu.VMEM((ROWS, D), jnp.bfloat16),
                pltpu.VMEM((D, E), jnp.bfloat16),
                pltpu.VMEM((ROWS, TOPK), jnp.int32),
                pltpu.SMEM((1,), jnp.int32),
                pltpu.VMEM((ROWS, E), jnp.float32),
                pltpu.VMEM((ROWS, E), jnp.float32),
                pltpu.VMEM((ROWS, E), jnp.bfloat16),
                pltpu.VMEM((ROWS, E), jnp.bfloat16),
                pltpu.VMEM((8, 8, HALF, 128), jnp.float32),
                pltpu.VMEM((8, 8, HALF, 128), jnp.float32),
                pltpu.VMEM((8, 8, HALF, 128), jnp.float32),
                *[pltpu.VMEM(p, jnp.float32) for p in pieces],
                *[pltpu.VMEM(p, jnp.float32) for p in pieces],
                pltpu.VMEM((2, 2, HALF, 128), jnp.float32),
                pltpu.VMEM((2, 3, 4, 8, E), jnp.float32),
                pltpu.SemaphoreType.DMA((3 + HCH,)),
                pltpu.SemaphoreType.DMA((8,)),
                pltpu.SemaphoreType.DMA((8,)),
                pltpu.SemaphoreType.DMA((6, 6)),
                pltpu.SemaphoreType.DMA((6, 6)),
                pltpu.SemaphoreType.DMA((2, 3)),
                pltpu.SemaphoreType.DMA((2, 3)),
                pltpu.SemaphoreType.DMA((3,)),
                pltpu.SemaphoreType.DMA((3,)),
            ],
            compiler_params=pltpu.CompilerParams(
                collective_id=0, has_side_effects=True, vmem_limit_bytes=60 * 1024 * 1024
            ),
        )(hidden, router_weight, expert_index, lengths)

    return jax.shard_map(
        shards,
        mesh=mesh,
        in_specs=(P(("seq", "ctx"), None), P(), P(("seq", "ctx"), None), P("seq")),
        out_specs=(P("ctx", None), P("seq")),
        check_vma=False,
    )
```

time: 212 us -> 68.7 us (0.32)
  waiting for transfers between devices: 126 us -> 0 us
  Pallas kernels: 0 us -> 62.1 us
  matrix products: 26 us -> 0 us
  blocking collectives: 15.2 us -> 0 us
  other arithmetic: 12.8 us -> 0 us
  between operations: 14.5 us -> 2.96 us
  starting transfers between devices: 11.3 us -> 0 us
  local copies, waits for them, and re-layouts: 5.72 us -> 3.39 us
    reduce_scatter x2 -> x0, waiting for transfers between devices: 89.9 us -> none  [sum_by_axis(): running = lax.psum_scatter(running, axis, scatter_dimension=0, tiled=True)]
    pallas_call x0 -> x1, Pallas kernels: none -> 62.1 us  [shards(): pl.pallas_call(kernel, out_shape=(jax.ShapeDtypeStruct((BLOCK, E), jnp.fl...]
    unnamed x4 -> x0, waiting for transfers between devices: 27.4 us -> none
    dot_general x2 -> x0, matrix products: 26 us -> none  [the longest x1 17.3 us: shards(): lax.dot_general(columns, grad_logits, (((0,), (0,)), ((), ())), precision...]
    all_to_all x1 -> x0, blocking collectives: 15.2 us -> none  [copy_for_each(): lax.all_to_all(jnp.broadcast_to(array[None], (size, *array.shape)), axis,...]
    reduce_sum x6 -> x0, other arithmetic: 12.8 us -> none  [the longest x1 10.9 us: shards(): jnp.sum((expert_index[:, :, None] == expert_ids).astype(jnp.float32), axi...]
    all_to_all x1 -> x0, starting transfers between devices: 11.2 us -> none  [copy_for_each(): lax.all_to_all(jnp.broadcast_to(array[None], (size, *array.shape)), axis,...]
    all_to_all x1 -> x0, waiting for transfers between devices: 8.67 us -> none  [copy_for_each(): lax.all_to_all(jnp.broadcast_to(array[None], (size, *array.shape)), axis,...]
  transfers between devices with their start and end apart: 4 -> 0, of which waited for: 4 -> 0; matrix products, arithmetic and copies ran while one was open for 0% -> 0% of each run, Pallas kernels for 0% -> 0%
where the time goes in v1:
time: 68.7 us; the launch traced here: 68.4 us
  Pallas kernels  62.1 us (90%)
  local copies, waits for them, and re-layouts  3.39 us (5%)
  between operations  2.96 us (4%)
    pallas_call x1, Pallas kernels, shards(): pl.pallas_call(kernel, out_shape=(jax.ShapeDtypeStruct((BLOCK, E), jnp.fl...  62.1 us
    unnamed x2, local copies, waits for them, and re-layouts  3.39 us

profile of v1, /device:TPU:1, one launch (start us, length us, event | category | flops | bytes accessed | tf_op | source)
XLA Modules:
  0.0 68.4 jit_solution(4280791297908144299)
XLA Ops:
  1.3 1.7 %copy.6.eidx = s32[1024,8]{1,0:T(8,128)} copy(s32[1024,8]{0,1:T(8,128)} %param.6) | data formatting | bytes 65536 | tf_op args[2]
  3.0 62.1 %shard_map.59 = (f32[224,256]{1,0:T(8,128)}, f32[1]{0:T(128)}) custom-call(bf16[1024,7168]{1,0:T(8,128)(2,1)} %hid.1, bf16[7168,256]{1,0:T(8,128)(2,1)} %wt.1, s32[1024,8]{1,0:T(8,128)} %copy.6.eidx, s32[1]{0:T(128)S(6)} %copy.9.lens), custom_call_target="tpu_custom_call" | custom-call | tf_op jit(solution)/shard_map/pallas_call | solution.py:301
  65.1 1.6 %copy.10 = f32[224,256]{1,0:T(8,128)} copy(f32[224,256]{1,0:T(8,128)} %get-tuple-element.4) | data formatting | bytes 458752

commit v2 on v1

v2 whole, which is shorter than its diff:
```python
import jax
import jax.numpy as jnp
from jax import lax
from jax.experimental import pallas as pl
from jax.experimental.pallas import tpu as pltpu
from jax.sharding import PartitionSpec as P

D = 7168
E = 256
TOPK = 8
ROWS = 1024
BLOCK = 224
HALF = BLOCK // 2
CHUNK = 4 * BLOCK
LOSS_SCALE = 65536.0
MESH = pl.DeviceIdType.MESH

SETS = (((0, 2), (1, 1), (2, 1), (3, 2), (4, 1), (5, 1)), ((0, 1), (1, 1), (2, 1), (3, 1), (4, 1), (5, 1)))
PIECES = tuple((t, n) for pieces in SETS for t, n in pieces)
TURN = tuple(t for t, _ in PIECES)
TILES = tuple(n for _, n in PIECES)
OFFSET = tuple(8 * sum(TILES[:p]) for p in range(len(PIECES)))
NP = len(PIECES)
SET_OF = (range(0, 6), range(6, 12))
SET_ROWS = ((0, 64), (64, 48))

HCH = 4
HROWS = ROWS // HCH
STRIP = 64


def turn(i, t):
    return (i, (i % 4) * 2 + i // 4, (i % 2) * 4 + i // 2)[t]


def place(p, j, b):
    t = TURN[p]
    return (turn(j, t), b) if t < 3 else (turn(b, t - 3), j)


def dimension(p, k):
    t = TURN[p]
    return (t + k) % 3 if t < 3 else 3 + (t + k) % 3


def kernel(hid, wt, eidx, lens, out, bal, *scratch):
    (h, w, idx, length, share, coef, ghi, glo, own, snd, got) = scratch[:11]
    acc, rb = scratch[11 : 11 + NP], scratch[11 + NP : 11 + 2 * NP]
    (fin, ar, in_sem, d2d_s, d2d_r, cube_s, cube_r, ar_s, ar_r, fin_s, fin_r) = scratch[11 + 2 * NP :]

    seq, ctx = lax.axis_index("seq"), lax.axis_index("ctx")
    core, zlo = seq % 2, seq // 2
    zh, x, y = ctx % 2, (ctx // 2) % 4, ctx // 8

    def device(y_, x_, zh_, zlo_, core_):
        return (zlo_ * 2 + core_, (y_ * 4 + x_) * 2 + zh_)

    def across(bits):
        y_, x_, zh_, zlo_ = y, x, zh, zlo
        if bits & 32:
            y_ = 3 - y_
        if bits & 16:
            y_ = y_ + 1 - 2 * (y_ % 2)
        if bits & 8:
            x_ = 3 - x_
        if bits & 4:
            x_ = x_ + 1 - 2 * (x_ % 2)
        if bits & 2:
            zh_, zlo_ = 1 - zh_, 1 - zlo_
        if bits & 1:
            zlo_ = 1 - zlo_
        return device(y_, x_, zh_, zlo_, core)

    cube = [across(32 >> d) for d in range(6)]
    far = ([across(r) for r in range(8)], [across(8 * r) for r in range(8)])
    other = device(y, x, zh, zlo, 1 - core)
    cross = device(y, x, zh, 1 - zlo, 1 - core)
    ring_x = [device(y, (x + d) % 4, zh, zlo, core) for d in (1, 2, 3)]
    ring_y = [device((y + d) % 4, x, zh, zlo, core) for d in (1, 2, 3)]
    pair_z = [device(y, x, 1 - zh, zlo, core)]
    stages = ((ring_x, x), (ring_y, y), (pair_z, zh))

    barrier = pltpu.get_barrier_semaphore()
    greeted = [across(r) for r in range(1, 8)] + [across(8 * r) for r in range(1, 8)] + pair_z + [other, cross]
    greeted += [device(y, (x + 2) % 4, zh, zlo, core), device((y + 2) % 4, x, zh, zlo, core)]
    for peer in greeted:
        pl.semaphore_signal(barrier, inc=1, device_id=peer, device_id_type=MESH)

    load_len = pltpu.make_async_copy(lens, length, in_sem.at[0])
    load_idx = pltpu.make_async_copy(eidx, idx, in_sem.at[1])
    load_w = [
        pltpu.make_async_copy(
            wt.at[:, pl.ds(pl.multiple_of(((core + e) % 2) * 128, 128), 128)], w.at[:, e * 128 : (e + 1) * 128],
            in_sem.at[2 + e],
        )
        for e in range(2)
    ]
    load_h = [
        pltpu.make_async_copy(hid.at[pl.ds(c * HROWS, HROWS)], h.at[pl.ds(c * HROWS, HROWS)], in_sem.at[4 + c])
        for c in range(HCH)
    ]
    load_len.start()
    load_idx.start()
    for e in range(2):
        load_w[e].start()
    for c in range(HCH):
        load_h[c].start()

    load_len.wait()
    load_idx.wait()
    live = length[0]
    first = ctx * ROWS

    hits = jnp.zeros((E, 128), jnp.float32)
    experts = (lax.broadcasted_iota(jnp.int32, (E, 128), 0) + core * 128) % E
    for i in range(ROWS // 128):
        block = idx[:, i * 128 : (i + 1) * 128]
        position = first + i * 128 + lax.broadcasted_iota(jnp.int32, block.shape, 1)
        block = jnp.where(position < live, block, -1)
        for k in range(TOPK):
            hits = hits + jnp.where(block[k : k + 1, :] == experts, 1.0, 0.0)
    counts = lax.dot_general(
        jnp.ones((8, 128), jnp.bfloat16), hits.astype(jnp.bfloat16), (((1,), (1,)), ((), ())),
        preferred_element_type=jnp.float32,
    )

    def ar_copy(kind, stage, peer, where):
        return pltpu.make_async_remote_copy(
            src_ref=ar.at[(kind, stage) + where],
            dst_ref=ar.at[(kind, stage) + where],
            send_sem=ar_s.at[kind, stage],
            recv_sem=ar_r.at[kind, stage],
            device_id=peer,
            device_id_type=MESH,
        )

    def ar_send(kind, stage, value):
        peers, mine = stages[stage]
        ar[kind, stage, mine] = value
        for peer in peers:
            ar_copy(kind, stage, peer, (mine,)).start()

    def ar_wait(kind, stage):
        peers, _ = stages[stage]
        n = len(peers)
        ar_copy(kind, stage, peers[0], (pl.ds(0, n),)).wait()
        total = ar[kind, stage, 0]
        for i in range(1, n + 1):
            total = total + ar[kind, stage, i]
        return total

    pl.semaphore_wait(barrier, len(greeted))
    ar_send(0, 0, counts)

    for e in range(2):
        load_w[e].wait()
    score_sum = jnp.zeros((8, E), jnp.float32)
    for c in range(HCH):
        rows = pl.ds(c * HROWS, HROWS)
        load_h[c].wait()
        share[rows, :] = jnp.dot(h[rows, :], w[...], preferred_element_type=jnp.float32)
        for r0 in range(c * HROWS, (c + 1) * HROWS, STRIP):
            rows = pl.ds(r0, STRIP)
            scores = jax.nn.sigmoid(share[rows, :])
            inverse = 1.0 / jnp.sum(scores, axis=1, keepdims=True)
            position = first + r0 + lax.broadcasted_iota(jnp.int32, (STRIP, 1), 0)
            valid = jnp.where(position < live, 1.0, 0.0)
            part = scores * inverse
            share[rows, :] = part
            part = part * valid
            coef[rows, :] = part * (1.0 - scores)
            score_sum = score_sum + part.reshape(STRIP // 8, 8, E).sum(axis=0)
        if c == 0:
            counts = ar_wait(0, 0)
            ar_send(0, 1, counts)
        if c == 2:
            counts = ar_wait(0, 1)
            ar_send(0, 2, counts)
    counts = ar_wait(0, 2)
    ar_send(1, 0, score_sum)

    tokens = live.astype(jnp.float32)
    fraction = E * counts[0:1] / (TOPK * tokens)
    weights = LOSS_SCALE * fraction / tokens
    for r0 in range(0, ROWS, 128):
        rows = pl.ds(r0, 128)
        weighted = jnp.sum(weights * share[rows, :], axis=1, keepdims=True)
        grad = (weights - weighted) * coef[rows, :]
        high = grad.astype(jnp.bfloat16)
        ghi[rows, :] = high
        glo[rows, :] = (grad - high.astype(jnp.float32)).astype(jnp.bfloat16)

    def d2d(j):
        return pltpu.make_async_remote_copy(
            src_ref=snd.at[j], dst_ref=got.at[j], send_sem=d2d_s.at[j], recv_sem=d2d_r.at[j],
            device_id=other, device_id_type=MESH,
        )

    def halving(s, k, where):
        return pltpu.make_async_remote_copy(
            src_ref=acc[s].at[where], dst_ref=rb[s].at[where], send_sem=cube_s.at[s, k], recv_sem=cube_r.at[s, k],
            device_id=cube[dimension(s, k)], device_id_type=MESH,
        )

    def upper(k):
        return (pl.ds(4 >> k, 4 >> k),)

    def straight(s, r):
        return pltpu.make_async_remote_copy(
            src_ref=acc[s].at[0, r], dst_ref=rb[s].at[0, r], send_sem=cube_s.at[s, 3], recv_sem=cube_r.at[s, 3],
            device_id=far[TURN[s] // 3][r], device_id_type=MESH,
        )

    def all_straight(s):
        return pltpu.make_async_remote_copy(
            src_ref=acc[s].at[0, pl.ds(1, 7)], dst_ref=rb[s].at[0, pl.ds(1, 7)], send_sem=cube_s.at[s, 3],
            recv_sem=cube_r.at[s, 3], device_id=far[TURN[s] // 3][1], device_id_type=MESH,
        )

    def final(i, where):
        return pltpu.make_async_remote_copy(
            src_ref=fin.at[(core, v) + where], dst_ref=fin.at[(core, v) + where], send_sem=fin_s.at[i],
            recv_sem=fin_r.at[i], device_id=(cube[5], cross, other)[i], device_id_type=MESH,
        )

    yhi, xhi = y // 2, x // 2
    ylo, xlo = (yhi + y) % 2, (xhi + x) % 2
    v = (zh + zlo) % 2

    def multiply(j):
        y_hi = (yhi + j // 4) % 2
        y_at = 2 * y_hi + (y_hi + ylo + (j // 2) % 2) % 2
        x_hi = (xhi + j) % 2
        start = (y_at * 2 + x_hi) * CHUNK
        for m in range(CHUNK // 128):
            part = h[:, pl.ds(pl.multiple_of(start + m * 128, 128), 128)]
            dims = (((0,), (0,)), ((), ()))
            made = lax.dot_general(part, ghi[...], dims, preferred_element_type=jnp.float32)
            made = made + lax.dot_general(part, glo[...], dims, preferred_element_type=jnp.float32)
            at = m * 128
            while at < (m + 1) * 128:
                to = min((at // HALF + 1) * HALF, (m + 1) * 128)
                piece = at // HALF
                b1 = (x_hi + piece // 4 + xlo) % 2
                b2 = (piece // 2 % 2 + zh) % 2
                b3 = (piece % 2 + v) % 2
                b = b1 * 4 + b2 * 2 + b3
                lo, size = at - piece * HALF, to - at
                own[j, b, lo : lo + size] = made[at - m * 128 : to - m * 128, :128]
                snd[j, b, lo : lo + size] = made[at - m * 128 : to - m * 128, 128:]
                at = to
        d2d(j).start()

    def gather(j):
        d2d(j).wait_recv()
        for b in range(8):
            total = own[j, b] + got[j, b]
            for s in range(NP):
                acc[s][place(s, j, b)] = total[OFFSET[s] : OFFSET[s] + 8 * TILES[s]]
        for s in range(NP):
            if TURN[s] >= 3:
                halving(s, 0, (pl.ds(4, 4), j)).start()
        for t, bit in ((0, j // 4), (1, (j // 2) % 2), (2, j % 2)):

            @pl.when(bit == 1)
            def _(t=t):
                for s in range(NP):
                    if TURN[s] == t:
                        halving(s, 0, (turn(j, t),)).start()

    def step(i, carry):
        @pl.when(i < 8)
        def _():
            multiply(7 - i)

        @pl.when(i > 0)
        def _():
            gather(8 - i)

        return carry

    lax.fori_loop(0, 9, step, 0)

    score_sum = ar_wait(1, 0)
    ar_send(1, 1, score_sum)

    for k in range(3):
        n = 4 >> k
        for s in range(NP):
            halving(s, k, upper(k)).wait_recv()
            acc[s][0:n] = acc[s][0:n] + rb[s][n : 2 * n]
            if k < 2:
                halving(s, k + 1, upper(k + 1)).start()
            else:
                for r in (7, 6, 5, 3, 4, 2, 1):
                    straight(s, r).start()
        if k == 1:
            score_sum = ar_wait(1, 1)
            ar_send(1, 2, score_sum)

    for half in range(2):
        for s in SET_OF[half]:
            all_straight(s).wait_recv()
            total = acc[s][0, 0]
            for r in range(1, 8):
                total = total + rb[s][0, r]
            fin[core, v, OFFSET[s] : OFFSET[s] + 8 * TILES[s]] = total
        for i in range(3):
            final(i, (pl.ds(*SET_ROWS[half]),)).start()

    score_sum = ar_wait(1, 2)
    mean_score = jnp.sum(score_sum, axis=0, keepdims=True) / tokens
    bal[0] = jnp.sum(fraction * mean_score)

    for s in range(NP):
        for k in range(3):
            halving(s, k, upper(k)).wait_send()
        all_straight(s).wait_send()
    for j in range(8):
        d2d(j).wait_send()
    for i in range(3):
        final(i, ()).wait()
    for e in range(2):
        for half in range(2):
            out[half * HALF : (half + 1) * HALF, e * 128 : (e + 1) * 128] = fin[e, half]


def solution(mesh):
    def shards(hidden, router_weight, expert_index, lengths):
        any_space = pl.BlockSpec(memory_space=pltpu.HBM)
        pieces = [(8, 8, 8 * t, 128) for t in TILES]
        return pl.pallas_call(
            kernel,
            out_shape=(jax.ShapeDtypeStruct((BLOCK, E), jnp.float32), jax.ShapeDtypeStruct((1,), jnp.float32)),
            in_specs=[any_space] * 4,
            out_specs=(pl.BlockSpec(memory_space=pltpu.VMEM), pl.BlockSpec(memory_space=pltpu.SMEM)),
            scratch_shapes=[
                pltpu.VMEM((ROWS, D), jnp.bfloat16),
                pltpu.VMEM((D, E), jnp.bfloat16),
                pltpu.VMEM((TOPK, ROWS), jnp.int32),
                pltpu.SMEM((1,), jnp.int32),
                pltpu.VMEM((ROWS, E), jnp.float32),
                pltpu.VMEM((ROWS, E), jnp.float32),
                pltpu.VMEM((ROWS, E), jnp.bfloat16),
                pltpu.VMEM((ROWS, E), jnp.bfloat16),
                pltpu.VMEM((8, 8, HALF, 128), jnp.float32),
                pltpu.VMEM((8, 8, HALF, 128), jnp.float32),
                pltpu.VMEM((8, 8, HALF, 128), jnp.float32),
                *[pltpu.VMEM(p, jnp.float32) for p in pieces],
                *[pltpu.VMEM(p, jnp.float32) for p in pieces],
                pltpu.VMEM((2, 2, HALF, 128), jnp.float32),
                pltpu.VMEM((2, 3, 4, 8, E), jnp.float32),
                pltpu.SemaphoreType.DMA((4 + HCH,)),
                pltpu.SemaphoreType.DMA((8,)),
                pltpu.SemaphoreType.DMA((8,)),
                pltpu.SemaphoreType.DMA((NP, 4)),
                pltpu.SemaphoreType.DMA((NP, 4)),
                pltpu.SemaphoreType.DMA((2, 3)),
                pltpu.SemaphoreType.DMA((2, 3)),
                pltpu.SemaphoreType.DMA((3,)),
                pltpu.SemaphoreType.DMA((3,)),
            ],
            compiler_params=pltpu.CompilerParams(
                collective_id=0, has_side_effects=True, vmem_limit_bytes=64487424
            ),
        )(hidden, router_weight, expert_index.T, lengths)

    return jax.shard_map(
        shards,
        mesh=mesh,
        in_specs=(P(("seq", "ctx"), None), P(), P(("seq", "ctx"), None), P("seq")),
        out_specs=(P("ctx", None), P("seq")),
        check_vma=False,
    )
```

time: 68.7 us -> 59.9 us (0.87)
  Pallas kernels: 62.1 us -> 55 us
  local copies, waits for them, and re-layouts: 3.39 us -> 1.64 us
    pallas_call x1, Pallas kernels: 62.1 us -> 55 us  [shards(): pl.pallas_call(kernel, out_shape=(jax.ShapeDtypeStruct((BLOCK, E), jnp.fl...]
    unnamed x2 -> x1, local copies, waits for them, and re-layouts: 3.39 us -> 1.64 us
where the time goes in v2:
time: 59.9 us; the launch traced here: 59.7 us
  Pallas kernels  55 us (92%)
  between operations  3.04 us (5%)
  local copies, waits for them, and re-layouts  1.64 us (3%)
    pallas_call x1, Pallas kernels, shards(): pl.pallas_call(kernel, out_shape=(jax.ShapeDtypeStruct((BLOCK, E), jnp.fl...  55 us
    unnamed x1, local copies, waits for them, and re-layouts  1.64 us

profile of v2, /device:TPU:1, one launch (start us, length us, event | category | flops | bytes accessed | tf_op | source)
XLA Modules:
  0.0 59.7 jit_solution(7559189301579783727)
XLA Ops:
  1.3 55.0 %shard_map.59 = (f32[224,256]{1,0:T(8,128)}, f32[1]{0:T(128)}) custom-call(bf16[1024,7168]{1,0:T(8,128)(2,1)} %hid.1, bf16[7168,256]{1,0:T(8,128)(2,1)} %wt.1, s32[8,1024]{1,0:T(8,128)} %bitcast.1, s32[1]{0:T(128)S(6)} %copy.8.lens), custom_call_target="tpu_custom_call" | custom-call | tf_op jit(solution)/shard_map/pallas_call | solution.py:332
  56.3 1.6 %copy.9 = f32[224,256]{1,0:T(8,128)} copy(f32[224,256]{1,0:T(8,128)} %get-tuple-element.4) | data formatting | bytes 458752

commit v3 on v2

--- a/solution.py
+++ b/solution.py
@@ -15,14 +15,16 @@
 LOSS_SCALE = 65536.0
 MESH = pl.DeviceIdType.MESH
 
-SETS = (((0, 2), (1, 1), (2, 1), (3, 2), (4, 1), (5, 1)), ((0, 1), (1, 1), (2, 1), (3, 1), (4, 1), (5, 1)))
-PIECES = tuple((t, n) for pieces in SETS for t, n in pieces)
-TURN = tuple(t for t, _ in PIECES)
-TILES = tuple(n for _, n in PIECES)
-OFFSET = tuple(8 * sum(TILES[:p]) for p in range(len(PIECES)))
-NP = len(PIECES)
-SET_OF = (range(0, 6), range(6, 12))
-SET_ROWS = ((0, 64), (64, 48))
+TILES = (3, 2, 2, 3, 2, 2)
+OFFSET = tuple(8 * sum(TILES[:p]) for p in range(6))
+FIRST, SECOND = (0, 1, 2), (3, 4, 5)
+ROWS_OF = ((0, OFFSET[3]), (OFFSET[3], HALF - OFFSET[3]))
+
+EVENTS = (
+    (8, 0, 3), (8, 1, 3), (8, 2, 3), (9, 2, 2), (10, 0, 2), (11, 1, 2), (12, 1, 1), (12, 2, 1), (13, 0, 1),
+    (16, 1, 0), (16, 2, 0), (17, 0, 0),
+)
+SOURCES = ((4, 2, 1), (5, 3), (6,), (7,))
 
 HCH = 4
 HROWS = ROWS // HCH
@@ -34,19 +36,17 @@
 
 
 def place(p, j, b):
-    t = TURN[p]
-    return (turn(j, t), b) if t < 3 else (turn(b, t - 3), j)
+    return (turn(j, p), b) if p < 3 else (turn(b, p - 3), j)
 
 
 def dimension(p, k):
-    t = TURN[p]
-    return (t + k) % 3 if t < 3 else 3 + (t + k) % 3
+    return (p + k) % 3 if p < 3 else 3 + (p + k) % 3
 
 
 def kernel(hid, wt, eidx, lens, out, bal, *scratch):
     (h, w, idx, length, share, coef, ghi, glo, own, snd, got) = scratch[:11]
-    acc, rb = scratch[11 : 11 + NP], scratch[11 + NP : 11 + 2 * NP]
-    (fin, ar, in_sem, d2d_s, d2d_r, cube_s, cube_r, ar_s, ar_r, fin_s, fin_r) = scratch[11 + 2 * NP :]
+    acc, rb = scratch[11:17], scratch[17:23]
+    (fin, ar, in_sem, d2d_s, d2d_r, one_s, one_r, two_s, two_r, far_s, far_r, ar_s, ar_r, fin_s, fin_r) = scratch[23:]
 
     seq, ctx = lax.axis_index("seq"), lax.axis_index("ctx")
     core, zlo = seq % 2, seq // 2
@@ -103,19 +103,18 @@
     load_idx.start()
     for e in range(2):
         load_w[e].start()
-    for c in range(HCH):
-        load_h[c].start()
+    load_h[0].start()
 
     load_len.wait()
     load_idx.wait()
     live = length[0]
-    first = ctx * ROWS
+    start_at = ctx * ROWS
 
     hits = jnp.zeros((E, 128), jnp.float32)
     experts = (lax.broadcasted_iota(jnp.int32, (E, 128), 0) + core * 128) % E
     for i in range(ROWS // 128):
         block = idx[:, i * 128 : (i + 1) * 128]
-        position = first + i * 128 + lax.broadcasted_iota(jnp.int32, block.shape, 1)
+        position = start_at + i * 128 + lax.broadcasted_iota(jnp.int32, block.shape, 1)
         block = jnp.where(position < live, block, -1)
         for k in range(TOPK):
             hits = hits + jnp.where(block[k : k + 1, :] == experts, 1.0, 0.0)
@@ -149,6 +148,7 @@
             total = total + ar[kind, stage, i]
         return total
 
+    load_h[1].start()
     pl.semaphore_wait(barrier, len(greeted))
     ar_send(0, 0, counts)
 
@@ -158,12 +158,14 @@
     for c in range(HCH):
         rows = pl.ds(c * HROWS, HROWS)
         load_h[c].wait()
+        if c + 2 < HCH:
+            load_h[c + 2].start()
         share[rows, :] = jnp.dot(h[rows, :], w[...], preferred_element_type=jnp.float32)
         for r0 in range(c * HROWS, (c + 1) * HROWS, STRIP):
             rows = pl.ds(r0, STRIP)
             scores = jax.nn.sigmoid(share[rows, :])
             inverse = 1.0 / jnp.sum(scores, axis=1, keepdims=True)
-            position = first + r0 + lax.broadcasted_iota(jnp.int32, (STRIP, 1), 0)
+            position = start_at + r0 + lax.broadcasted_iota(jnp.int32, (STRIP, 1), 0)
             valid = jnp.where(position < live, 1.0, 0.0)
             part = scores * inverse
             share[rows, :] = part
@@ -196,25 +198,30 @@
             device_id=other, device_id_type=MESH,
         )
 
-    def halving(s, k, where):
-        return pltpu.make_async_remote_copy(
-            src_ref=acc[s].at[where], dst_ref=rb[s].at[where], send_sem=cube_s.at[s, k], recv_sem=cube_r.at[s, k],
-            device_id=cube[dimension(s, k)], device_id_type=MESH,
-        )
-
-    def upper(k):
-        return (pl.ds(4 >> k, 4 >> k),)
-
-    def straight(s, r):
-        return pltpu.make_async_remote_copy(
-            src_ref=acc[s].at[0, r], dst_ref=rb[s].at[0, r], send_sem=cube_s.at[s, 3], recv_sem=cube_r.at[s, 3],
-            device_id=far[TURN[s] // 3][r], device_id_type=MESH,
-        )
-
-    def all_straight(s):
-        return pltpu.make_async_remote_copy(
-            src_ref=acc[s].at[0, pl.ds(1, 7)], dst_ref=rb[s].at[0, pl.ds(1, 7)], send_sem=cube_s.at[s, 3],
-            recv_sem=cube_r.at[s, 3], device_id=far[TURN[s] // 3][1], device_id_type=MESH,
+    def first(p, k, r):
+        return pltpu.make_async_remote_copy(
+            src_ref=acc[p].at[r], dst_ref=rb[p].at[r], send_sem=one_s.at[p, r], recv_sem=one_r.at[p, r],
+            device_id=cube[dimension(p, k)], device_id_type=MESH,
+        )
+
+    def second(p, k, j):
+        where = (pl.ds(4 >> k, 4 >> k), j)
+        return pltpu.make_async_remote_copy(
+            src_ref=acc[p].at[where], dst_ref=rb[p].at[where], send_sem=two_s.at[p - 3, k, j],
+            recv_sem=two_r.at[p - 3, k, j], device_id=cube[dimension(p, k)], device_id_type=MESH,
+        )
+
+    def straight(p, r):
+        return pltpu.make_async_remote_copy(
+            src_ref=acc[p].at[0, r], dst_ref=rb[p].at[0, r], send_sem=far_s.at[p], recv_sem=far_r.at[p],
+            device_id=far[p // 3][r], device_id_type=MESH,
+        )
+
+    def all_straight(p):
+        where = (0, pl.ds(1, 7))
+        return pltpu.make_async_remote_copy(
+            src_ref=acc[p].at[where], dst_ref=rb[p].at[where], send_sem=far_s.at[p], recv_sem=far_r.at[p],
+            device_id=far[p // 3][1], device_id_type=MESH,
         )
 
     def final(i, where):
@@ -255,67 +262,110 @@
         d2d(j).wait_recv()
         for b in range(8):
             total = own[j, b] + got[j, b]
-            for s in range(NP):
+            for s in range(6):
                 acc[s][place(s, j, b)] = total[OFFSET[s] : OFFSET[s] + 8 * TILES[s]]
-        for s in range(NP):
-            if TURN[s] >= 3:
-                halving(s, 0, (pl.ds(4, 4), j)).start()
-        for t, bit in ((0, j // 4), (1, (j // 2) % 2), (2, j % 2)):
+        for p in SECOND:
+            second(p, 0, j).start()
+        for p, bit in ((0, j // 4), (1, (j // 2) % 2), (2, j % 2)):
 
             @pl.when(bit == 1)
-            def _(t=t):
-                for s in range(NP):
-                    if TURN[s] == t:
-                        halving(s, 0, (turn(j, t),)).start()
+            def _(p=p):
+                first(p, 0, turn(j, p)).start()
+
+    def advance(p, r):
+        total = acc[p][r]
+        for source in SOURCES[r]:
+            first(p, 0 if source >= 4 else 1 if source >= 2 else 2, source).wait_recv()
+            total = total + rb[p][source]
+        acc[p][r] = total
+        if r > 0:
+            first(p, 1 if r >= 2 else 2, r).start()
+        else:
+            for b in (7, 6, 5, 3, 4, 2, 1):
+                straight(p, b).start()
 
     def step(i, carry):
         @pl.when(i < 8)
         def _():
             multiply(7 - i)
 
-        @pl.when(i > 0)
-        def _():
-            gather(8 - i)
+        @pl.when((i > 1) & (i < 10))
+        def _():
+            gather(9 - i)
+
+        @pl.when(i == 5)
+        def _():
+            ar_send(1, 1, ar_wait(1, 0))
+
+        for at in sorted({at for at, _, _ in EVENTS}):
+
+            @pl.when(i == at)
+            def _(at=at):
+                for at_, p, r in EVENTS:
+                    if at_ == at:
+                        advance(p, r)
+
+        @pl.when((i > 5) & (i < 14))
+        def _():
+            j = 13 - i
+            for p in SECOND:
+                second(p, 0, j).wait_recv()
+                acc[p][0:4, j] = acc[p][0:4, j] + rb[p][4:8, j]
+                second(p, 1, j).start()
+
+        @pl.when((i > 8) & (i < 17))
+        def _():
+            j = 16 - i
+            for p in SECOND:
+                second(p, 1, j).wait_recv()
+                acc[p][0:2, j] = acc[p][0:2, j] + rb[p][2:4, j]
+                second(p, 2, j).start()
+
+        @pl.when(i == 10)
+        def _():
+            ar_send(1, 2, ar_wait(1, 1))
+
+        @pl.when(i > 11)
+        def _():
+            j = 19 - i
+            for p in SECOND:
+                second(p, 2, j).wait_recv()
+                acc[p][0, j] = acc[p][0, j] + rb[p][1, j]
+
+        for r in range(1, 8):
+
+            @pl.when(i == 19 - r)
+            def _(r=r):
+                for p in SECOND:
+                    straight(p, r).start()
 
         return carry
 
-    lax.fori_loop(0, 9, step, 0)
-
-    score_sum = ar_wait(1, 0)
-    ar_send(1, 1, score_sum)
-
-    for k in range(3):
-        n = 4 >> k
-        for s in range(NP):
-            halving(s, k, upper(k)).wait_recv()
-            acc[s][0:n] = acc[s][0:n] + rb[s][n : 2 * n]
-            if k < 2:
-                halving(s, k + 1, upper(k + 1)).start()
-            else:
-                for r in (7, 6, 5, 3, 4, 2, 1):
-                    straight(s, r).start()
-        if k == 1:
-            score_sum = ar_wait(1, 1)
-            ar_send(1, 2, score_sum)
-
-    for half in range(2):
-        for s in SET_OF[half]:
-            all_straight(s).wait_recv()
-            total = acc[s][0, 0]
+    lax.fori_loop(0, 20, step, 0)
+
+    for half, pieces in enumerate((FIRST, SECOND)):
+        for p in pieces:
+            all_straight(p).wait_recv()
+            total = acc[p][0, 0]
             for r in range(1, 8):
-                total = total + rb[s][0, r]
-            fin[core, v, OFFSET[s] : OFFSET[s] + 8 * TILES[s]] = total
+                total = total + rb[p][0, r]
+            fin[core, v, OFFSET[p] : OFFSET[p] + 8 * TILES[p]] = total
         for i in range(3):
-            final(i, (pl.ds(*SET_ROWS[half]),)).start()
+            final(i, (pl.ds(*ROWS_OF[half]),)).start()
 
     score_sum = ar_wait(1, 2)
     mean_score = jnp.sum(score_sum, axis=0, keepdims=True) / tokens
     bal[0] = jnp.sum(fraction * mean_score)
 
-    for s in range(NP):
+    for p in FIRST:
+        for r in range(1, 8):
+            first(p, 0, r).wait_send()
+    for p in SECOND:
         for k in range(3):
-            halving(s, k, upper(k)).wait_send()
-        all_straight(s).wait_send()
+            for j in range(8):
+                second(p, k, j).wait_send()
+    for p in range(6):
+        all_straight(p).wait_send()
     for j in range(8):
         d2d(j).wait_send()
     for i in range(3):
@@ -331,7 +381,7 @@
         pieces = [(8, 8, 8 * t, 128) for t in TILES]
         return pl.pallas_call(
             kernel,
-            out_shape=(jax.ShapeDtypeStruct((BLOCK, E), jnp.float32), jax.ShapeDtypeStruct((1,), jnp.float32)),
+            out_shape=(pltpu.VMEM((BLOCK, E), jnp.float32), jax.ShapeDtypeStruct((1,), jnp.float32)),
             in_specs=[any_space] * 4,
             out_specs=(pl.BlockSpec(memory_space=pltpu.VMEM), pl.BlockSpec(memory_space=pltpu.SMEM)),
             scratch_shapes=[
@@ -353,8 +403,12 @@
                 pltpu.SemaphoreType.DMA((4 + HCH,)),
                 pltpu.SemaphoreType.DMA((8,)),
                 pltpu.SemaphoreType.DMA((8,)),
-                pltpu.SemaphoreType.DMA((NP, 4)),
-                pltpu.SemaphoreType.DMA((NP, 4)),
+                pltpu.SemaphoreType.DMA((3, 8)),
+                pltpu.SemaphoreType.DMA((3, 8)),
+                pltpu.SemaphoreType.DMA((3, 3, 8)),
+                pltpu.SemaphoreType.DMA((3, 3, 8)),
+                pltpu.SemaphoreType.DMA((6,)),
+                pltpu.SemaphoreType.DMA((6,)),
                 pltpu.SemaphoreType.DMA((2, 3)),
                 pltpu.SemaphoreType.DMA((2, 3)),
                 pltpu.SemaphoreType.DMA((3,)),

time: 59.9 us -> 57 us (0.952)
  Pallas kernels: 55 us -> 53.2 us
  local copies, waits for them, and re-layouts: 1.64 us -> 0.69 us
    pallas_call x1, Pallas kernels: 55 us -> 53.2 us  [shards(): pl.pallas_call(kernel, out_shape=(pltpu.VMEM((BLOCK, E), jnp.float32), ja...]
    unnamed x1, local copies, waits for them, and re-layouts: 1.64 us -> 0.69 us
where the time goes in v3:
time: 57 us; the launch traced here: 56.9 us
  Pallas kernels  53.2 us (93%)
  between operations  2.97 us (5%)
  local copies, waits for them, and re-layouts  0.69 us (1%)
    pallas_call x1, Pallas kernels, shards(): pl.pallas_call(kernel, out_shape=(pltpu.VMEM((BLOCK, E), jnp.float32), ja...  53.2 us

profile of v3, /device:TPU:1, one launch (start us, length us, event | category | flops | bytes accessed | tf_op | source)
XLA Modules:
  0.0 56.9 jit_solution(6020257033823385065)
XLA Ops:
  1.3 53.2 %shard_map.59 = (f32[224,256]{1,0:T(8,128)S(1)}, f32[1]{0:T(128)}) custom-call(bf16[1024,7168]{1,0:T(8,128)(2,1)} %hid.1, bf16[7168,256]{1,0:T(8,128)(2,1)} %wt.1, s32[8,1024]{1,0:T(8,128)} %bitcast.1, s32[1]{0:T(128)S(6)} %copy.9.lens), custom_call_target="tpu_custom_call" | custom-call | tf_op jit(solution)/shard_map/pallas_call | solution.py:382
  54.5 0.7 %copy.8 = f32[224,256]{1,0:T(8,128)} copy(f32[224,256]{1,0:T(8,128)S(1)} %get-tuple-element.2) | data formatting | bytes 458752

commit v4 on v3

--- a/solution.py
+++ b/solution.py
@@ -21,8 +21,8 @@
 ROWS_OF = ((0, OFFSET[3]), (OFFSET[3], HALF - OFFSET[3]))
 
 EVENTS = (
-    (8, 0, 3), (8, 1, 3), (8, 2, 3), (9, 2, 2), (10, 0, 2), (11, 1, 2), (12, 1, 1), (12, 2, 1), (13, 0, 1),
-    (16, 1, 0), (16, 2, 0), (17, 0, 0),
+    (6, 1, 3), (7, 2, 3), (8, 0, 3), (8, 2, 2), (10, 0, 2), (10, 1, 2), (11, 1, 1), (11, 2, 1), (12, 0, 1),
+    (14, 1, 0), (14, 2, 0), (15, 0, 0),
 )
 SOURCES = ((4, 2, 1), (5, 3), (6,), (7,))
 
@@ -75,14 +75,13 @@
     far = ([across(r) for r in range(8)], [across(8 * r) for r in range(8)])
     other = device(y, x, zh, zlo, 1 - core)
     cross = device(y, x, zh, 1 - zlo, 1 - core)
-    ring_x = [device(y, (x + d) % 4, zh, zlo, core) for d in (1, 2, 3)]
+    plane = [device(y, (x + d // 2) % 4, (zh + d) % 2, zlo, core) for d in range(1, 8)]
     ring_y = [device((y + d) % 4, x, zh, zlo, core) for d in (1, 2, 3)]
-    pair_z = [device(y, x, 1 - zh, zlo, core)]
-    stages = ((ring_x, x), (ring_y, y), (pair_z, zh))
+    stages = ((plane, x * 2 + zh), (ring_y, y))
 
     barrier = pltpu.get_barrier_semaphore()
-    greeted = [across(r) for r in range(1, 8)] + [across(8 * r) for r in range(1, 8)] + pair_z + [other, cross]
-    greeted += [device(y, (x + 2) % 4, zh, zlo, core), device((y + 2) % 4, x, zh, zlo, core)]
+    greeted = plane + ring_y + [across(r) for r in (1, 2, 3, 5, 6, 7)] + [across(8 * r) for r in (3, 5, 6, 7)]
+    greeted += [other, cross]
     for peer in greeted:
         pl.semaphore_signal(barrier, inc=1, device_id=peer, device_id_type=MESH)
 
@@ -150,7 +149,7 @@
 
     load_h[1].start()
     pl.semaphore_wait(barrier, len(greeted))
-    ar_send(0, 0, counts)
+    ar_send(0, 0, counts[0:1])
 
     for e in range(2):
         load_w[e].wait()
@@ -172,17 +171,14 @@
             part = part * valid
             coef[rows, :] = part * (1.0 - scores)
             score_sum = score_sum + part.reshape(STRIP // 8, 8, E).sum(axis=0)
-        if c == 0:
+        if c == 1:
             counts = ar_wait(0, 0)
             ar_send(0, 1, counts)
-        if c == 2:
-            counts = ar_wait(0, 1)
-            ar_send(0, 2, counts)
-    counts = ar_wait(0, 2)
-    ar_send(1, 0, score_sum)
+    counts = ar_wait(0, 1)
+    ar_send(1, 0, jnp.sum(score_sum, axis=0, keepdims=True))
 
     tokens = live.astype(jnp.float32)
-    fraction = E * counts[0:1] / (TOPK * tokens)
+    fraction = E * counts / (TOPK * tokens)
     weights = LOSS_SCALE * fraction / tokens
     for r0 in range(0, ROWS, 128):
         rows = pl.ds(r0, 128)
@@ -293,7 +289,7 @@
         def _():
             gather(9 - i)
 
-        @pl.when(i == 5)
+        @pl.when(i == 7)
         def _():
             ar_send(1, 1, ar_wait(1, 0))
 
@@ -305,43 +301,39 @@
                     if at_ == at:
                         advance(p, r)
 
-        @pl.when((i > 5) & (i < 14))
-        def _():
-            j = 13 - i
+        @pl.when((i > 4) & (i < 13))
+        def _():
+            j = 12 - i
             for p in SECOND:
                 second(p, 0, j).wait_recv()
                 acc[p][0:4, j] = acc[p][0:4, j] + rb[p][4:8, j]
                 second(p, 1, j).start()
 
-        @pl.when((i > 8) & (i < 17))
-        def _():
-            j = 16 - i
+        @pl.when((i > 7) & (i < 16))
+        def _():
+            j = 15 - i
             for p in SECOND:
                 second(p, 1, j).wait_recv()
                 acc[p][0:2, j] = acc[p][0:2, j] + rb[p][2:4, j]
                 second(p, 2, j).start()
 
-        @pl.when(i == 10)
-        def _():
-            ar_send(1, 2, ar_wait(1, 1))
-
-        @pl.when(i > 11)
-        def _():
-            j = 19 - i
+        @pl.when((i > 10) & (i < 19))
+        def _():
+            j = 18 - i
             for p in SECOND:
                 second(p, 2, j).wait_recv()
                 acc[p][0, j] = acc[p][0, j] + rb[p][1, j]
 
         for r in range(1, 8):
 
-            @pl.when(i == 19 - r)
+            @pl.when(i == 18 - r)
             def _(r=r):
                 for p in SECOND:
                     straight(p, r).start()
 
         return carry
 
-    lax.fori_loop(0, 20, step, 0)
+    lax.fori_loop(0, 19, step, 0)
 
     for half, pieces in enumerate((FIRST, SECOND)):
         for p in pieces:
@@ -353,8 +345,8 @@
         for i in range(3):
             final(i, (pl.ds(*ROWS_OF[half]),)).start()
 
-    score_sum = ar_wait(1, 2)
-    mean_score = jnp.sum(score_sum, axis=0, keepdims=True) / tokens
+    score_sum = ar_wait(1, 1)
+    mean_score = score_sum / tokens
     bal[0] = jnp.sum(fraction * mean_score)
 
     for p in FIRST:
@@ -399,7 +391,7 @@
                 *[pltpu.VMEM(p, jnp.float32) for p in pieces],
                 *[pltpu.VMEM(p, jnp.float32) for p in pieces],
                 pltpu.VMEM((2, 2, HALF, 128), jnp.float32),
-                pltpu.VMEM((2, 3, 4, 8, E), jnp.float32),
+                pltpu.VMEM((2, 2, 8, 1, E), jnp.float32),
                 pltpu.SemaphoreType.DMA((4 + HCH,)),
                 pltpu.SemaphoreType.DMA((8,)),
                 pltpu.SemaphoreType.DMA((8,)),
@@ -409,8 +401,8 @@
                 pltpu.SemaphoreType.DMA((3, 3, 8)),
                 pltpu.SemaphoreType.DMA((6,)),
                 pltpu.SemaphoreType.DMA((6,)),
-                pltpu.SemaphoreType.DMA((2, 3)),
-                pltpu.SemaphoreType.DMA((2, 3)),
+                pltpu.SemaphoreType.DMA((2, 2)),
+                pltpu.SemaphoreType.DMA((2, 2)),
                 pltpu.SemaphoreType.DMA((3,)),
                 pltpu.SemaphoreType.DMA((3,)),
             ],

time: 57 us -> 55.2 us (0.968)
  Pallas kernels: 53.2 us -> 51.4 us
    pallas_call x1, Pallas kernels: 53.2 us -> 51.4 us  [shards(): pl.pallas_call(kernel, out_shape=(pltpu.VMEM((BLOCK, E), jnp.float32), ja...]
where the time goes in v4:
time: 55.2 us; the launch traced here: 55.1 us
  Pallas kernels  51.4 us (93%)
  between operations  2.97 us (5%)
  local copies, waits for them, and re-layouts  0.69 us (1%)
    pallas_call x1, Pallas kernels, shards(): pl.pallas_call(kernel, out_shape=(pltpu.VMEM((BLOCK, E), jnp.float32), ja...  51.4 us

profile of v4, /device:TPU:1, one launch (start us, length us, event | category | flops | bytes accessed | tf_op | source)
XLA Modules:
  0.0 55.1 jit_solution(16399671034227954282)
XLA Ops:
  1.3 51.4 %shard_map.59 = (f32[224,256]{1,0:T(8,128)S(1)}, f32[1]{0:T(128)}) custom-call(bf16[1024,7168]{1,0:T(8,128)(2,1)} %hid.1, bf16[7168,256]{1,0:T(8,128)(2,1)} %wt.1, s32[8,1024]{1,0:T(8,128)} %bitcast.1, s32[1]{0:T(128)S(6)} %copy.9.lens), custom_call_target="tpu_custom_call" | custom-call | tf_op jit(solution)/shard_map/pallas_call | solution.py:374
  52.7 0.7 %copy.8 = f32[224,256]{1,0:T(8,128)} copy(f32[224,256]{1,0:T(8,128)S(1)} %get-tuple-element.2) | data formatting | bytes 458752

commit v5 on v4

--- a/solution.py
+++ b/solution.py
@@ -342,8 +342,8 @@
             for r in range(1, 8):
                 total = total + rb[p][0, r]
             fin[core, v, OFFSET[p] : OFFSET[p] + 8 * TILES[p]] = total
-        for i in range(3):
-            final(i, (pl.ds(*ROWS_OF[half]),)).start()
+            for i in range(3):
+                final(i, (pl.ds(OFFSET[p], 8 * TILES[p]),)).start()
 
     score_sum = ar_wait(1, 1)
     mean_score = score_sum / tokens

time: 55.2 us -> 55.3 us (level)
  no operation moved by 1% of the time
where the time goes in v5:
time: 55.3 us; the launch traced here: 55.1 us
  Pallas kernels  51.5 us (93%)
  between operations  2.97 us (5%)
  local copies, waits for them, and re-layouts  0.69 us (1%)
    pallas_call x1, Pallas kernels, shards(): pl.pallas_call(kernel, out_shape=(pltpu.VMEM((BLOCK, E), jnp.float32), ja...  51.5 us

profile of v5, /device:TPU:1, one launch (start us, length us, event | category | flops | bytes accessed | tf_op | source)
XLA Modules:
  0.0 55.1 jit_solution(16112668088807404990)
XLA Ops:
  1.3 51.5 %shard_map.59 = (f32[224,256]{1,0:T(8,128)S(1)}, f32[1]{0:T(128)}) custom-call(bf16[1024,7168]{1,0:T(8,128)(2,1)} %hid.1, bf16[7168,256]{1,0:T(8,128)(2,1)} %wt.1, s32[8,1024]{1,0:T(8,128)} %bitcast.1, s32[1]{0:T(128)S(6)} %copy.9.lens), custom_call_target="tpu_custom_call" | custom-call | tf_op jit(solution)/shard_map/pallas_call | solution.py:374
  52.7 0.7 %copy.8 = f32[224,256]{1,0:T(8,128)} copy(f32[224,256]{1,0:T(8,128)S(1)} %get-tuple-element.2) | data formatting | bytes 458752
